TPU v7x, 32 devices: a whole 2x2x4 slice. The times are simulated.
32 devices in a mesh: fsdp: 2 (over y), ctx: 4 (over x, core), tp: 4 (over z).
Axes of the slice: x: 2, y: 2, z: 4, core: 2. Of those that a mesh axis runs over, the one named last changes fastest.
Arguments:
- block_input: bfloat16 [4, 2048, 1024], P('fsdp', 'ctx'), may hold values from -6 to 6
- positions: int32 [3, 4, 2048], P(None, 'fsdp', 'ctx'), may hold values from 0 to 15
- w_qkv: bfloat16 [3, 1024, 1024], P(None, 'fsdp', 'tp'), may hold values from -0.1875 to 0.1875
- b_qkv: float32 [3, 1024], P(None, 'tp'), may hold values from -3 to 3
- w_proj: bfloat16 [1024, 1024], P('tp', 'fsdp'), may hold values from -1 to 1
- w_up: bfloat16 [1024, 4096], P('fsdp', 'tp'), may hold values from -0.1875 to 0.1875
- b_up: float32 [4096], P('tp'), may hold values from -3 to 3
- w_down: bfloat16 [4096, 1024], P('tp', 'fsdp'), may hold values from -0.09375 to 0.09375
- norm_gains: float32 [2, 1024], replicated, may hold values from 0.5 to 1.5
- norm_shifts: float32 [2, 1024], replicated, may hold values from -2 to 2
- out_shifts: float32 [2, 1024], replicated, may hold values from -2 to 2
- grad_out: bfloat16 [4, 2048, 1024], P('fsdp', 'ctx'), may hold values from -6 to 6
Outputs:
- block_output: bfloat16 [4, 2048, 1024], P('fsdp', 'ctx')
- grad_input: float32 [4, 2048, 1024], P('fsdp', 'ctx')
- grad_w_qkv: float32 [3, 1024, 1024], P(None, 'fsdp', 'tp')
- grad_b_qkv: float32 [3, 1024], P(None, 'tp')
- grad_w_proj: float32 [1024, 1024], P('tp', 'fsdp')
- grad_w_up: float32 [1024, 4096], P('fsdp', 'tp')
- grad_b_up: float32 [4096], P('tp')
- grad_w_down: float32 [4096, 1024], P('tp', 'fsdp')
- grad_gains: float32 [2, 1024], replicated
- grad_shifts: float32 [2, 1024], replicated
- grad_out_shifts: float32 [2, 1024], replicated
Inputs may be any that keep to these rules, and one draw needn't show every extreme that they name: `positions`: each token's time, height and width index in its clip.
All inputs are finite; a program needn't handle non-finite values.
Results may differ from a plain program's by a relative error of at most 0.02.
Values may be sent and summed in bfloat16 or wider, within the bound.
A program may use at most 128 MiB of HBM per device.

v0:
```python
from functools import partial
import jax
import jax.numpy as jnp
from jax import lax
from jax.sharding import PartitionSpec as P

HD = 64
LEN = 2048
ROT = 20
QBLK = 512
EPSILON = 1e-06


def layer_norm(values, gain_vec, shift_vec):
    center = values - jnp.mean(values, axis=-1, keepdims=True)
    spread = jnp.mean(center * center, axis=-1, keepdims=True)
    return center * lax.rsqrt(spread + EPSILON) * gain_vec + shift_vec


def rotary_tables(position_rows):
    half_rot = ROT // 2
    freqs = 10000.0 ** (-2.0 * jnp.arange(half_rot, dtype=jnp.float32) / ROT)
    angles = position_rows.astype(jnp.float32)[:, :, None] * freqs[None, None, :]
    return (jnp.cos(angles), jnp.sin(angles))


def rotary(values, cos_table, sin_table):
    half_rot = ROT // 2
    pieces = []
    for dim_index in range(3):
        offset_at = dim_index * ROT
        first_half = values[..., offset_at : offset_at + half_rot]
        second_half = values[..., offset_at + half_rot : offset_at + ROT]
        cos_part = cos_table[dim_index][:, None, :]
        sin_part = sin_table[dim_index][:, None, :]
        pieces.append(first_half * cos_part - second_half * sin_part)
        pieces.append(second_half * cos_part + first_half * sin_part)
    pieces.append(values[..., 3 * ROT :])
    return jnp.concatenate(pieces, axis=-1)


def contract_rows(left_mat, right_mat):
    return lax.dot_general(
        left_mat, right_mat, (((0,), (0,)), ((), ())), preferred_element_type=jnp.float32
    )


def contract_cols(left_mat, right_mat):
    return lax.dot_general(
        left_mat, right_mat, (((1,), (1,)), ((), ())), preferred_element_type=jnp.float32
    )


def tp_whole(partial_sum):
    return lax.psum(partial_sum.astype(jnp.bfloat16), "tp").astype(jnp.float32)


def attend_group(operands):
    queries, keys_all, values_all = operands
    score_factor = HD ** (-0.5)

    def attend_block(query_block):
        scores = (
            jnp.einsum("qe,ke->qk", query_block, keys_all, preferred_element_type=jnp.float32)
            * score_factor
        )
        largest = jnp.max(scores, axis=-1, keepdims=True)
        expon = jnp.exp(scores - largest)
        totals = jnp.sum(expon, axis=-1, keepdims=True)
        probs = expon / totals
        block_out = jnp.dot(
            probs.astype(jnp.bfloat16), values_all, preferred_element_type=jnp.float32
        )
        return (block_out.astype(jnp.bfloat16), (largest + jnp.log(totals))[:, 0])

    return lax.map(attend_block, queries.reshape(LEN // QBLK, QBLK, HD))


def backward_group(operands):
    queries, keys_all, values_all, grad_attended, log_totals = operands
    score_factor = HD ** (-0.5)

    def back_block(carry, block_items):
        grad_keys, grad_values = carry
        query_block, grad_block, log_block = block_items
        scores = (
            jnp.einsum("qe,ke->qk", query_block, keys_all, preferred_element_type=jnp.float32)
            * score_factor
        )
        probs = jnp.exp(scores - log_block[:, None])
        probs_low = probs.astype(jnp.bfloat16)
        grad_probs = jnp.einsum(
            "qe,ke->qk", grad_block, values_all, preferred_element_type=jnp.float32
        )
        inner = jnp.sum(probs * grad_probs, axis=-1, keepdims=True)
        grad_scores = (probs * (grad_probs - inner)).astype(jnp.bfloat16)
        grad_query = (
            jnp.dot(grad_scores, keys_all, preferred_element_type=jnp.float32) * score_factor
        )
        grad_keys = grad_keys + contract_rows(grad_scores, query_block) * score_factor
        grad_values = grad_values + contract_rows(probs_low, grad_block)
        return ((grad_keys, grad_values), grad_query)

    zeros_kv = jnp.zeros((LEN, HD), jnp.float32)
    block_count = LEN // QBLK
    items = (
        queries.reshape(block_count, QBLK, HD),
        grad_attended.reshape(block_count, QBLK, HD),
        log_totals,
    )
    (grad_keys, grad_values), grad_queries = lax.scan(back_block, (zeros_kv, zeros_kv), items)
    return (grad_queries.reshape(LEN, HD), grad_keys, grad_values)


def shards(
    block_input,
    positions,
    w_qkv,
    b_qkv,
    w_proj,
    w_up,
    b_up,
    w_down,
    norm_gains,
    norm_shifts,
    out_shifts,
    grad_out,
):
    clip_count, local_len, width = block_input.shape
    row_count = clip_count * local_len
    ctx_count = lax.axis_size("ctx")
    local_width = w_qkv.shape[2]
    group_heads = local_width // ctx_count // HD
    group_count = clip_count * group_heads
    inputs = block_input.reshape(row_count, width).astype(jnp.float32)
    full_qkv, full_proj, full_up, full_down = (
        lax.all_gather(w_qkv, "fsdp", axis=1, tiled=True),
        lax.all_gather(w_proj, "fsdp", axis=1, tiled=True),
        lax.all_gather(w_up, "fsdp", axis=0, tiled=True),
        lax.all_gather(w_down, "fsdp", axis=1, tiled=True),
    )
    cos_table, sin_table = rotary_tables(positions.reshape(3, row_count))
    normed_one = layer_norm(inputs, norm_gains[0], norm_shifts[0])
    normed_one_low = normed_one.astype(jnp.bfloat16)
    projected = (
        jnp.einsum("rd,cde->cre", normed_one_low, full_qkv, preferred_element_type=jnp.float32)
        + b_qkv[:, None, :]
    )
    head_shape = (row_count, local_width // HD, HD)
    queries_rot = rotary(projected[0].reshape(head_shape), cos_table, sin_table).reshape(
        row_count, local_width
    )
    keys_rot = rotary(projected[1].reshape(head_shape), cos_table, sin_table).reshape(
        row_count, local_width
    )
    token_qkv = (
        jnp.stack([queries_rot, keys_rot, projected[2]])
        .astype(jnp.bfloat16)
        .reshape(3, clip_count, local_len, local_width)
    )
    head_qkv = lax.all_to_all(token_qkv, "ctx", split_axis=3, concat_axis=2, tiled=True)
    full_len = head_qkv.shape[2]
    grouped = (
        head_qkv.reshape(3, clip_count, full_len, group_heads, HD)
        .transpose(0, 1, 3, 2, 4)
        .reshape(3, group_count, full_len, HD)
    )
    attended, log_totals = lax.map(attend_group, (grouped[0], grouped[1], grouped[2]))
    attended = (
        attended.reshape(clip_count, group_heads, full_len, HD)
        .transpose(0, 2, 1, 3)
        .reshape(clip_count, full_len, group_heads * HD)
    )
    token_attended = lax.all_to_all(
        attended, "ctx", split_axis=1, concat_axis=2, tiled=True
    ).reshape(row_count, local_width)
    attn_part = jnp.dot(token_attended, full_proj, preferred_element_type=jnp.float32)
    residual = inputs + tp_whole(attn_part) + out_shifts[0]
    normed_two_low = layer_norm(residual, norm_gains[1], norm_shifts[1]).astype(jnp.bfloat16)
    pre_act = jnp.dot(normed_two_low, full_up, preferred_element_type=jnp.float32) + b_up
    act_low = jax.nn.gelu(pre_act, approximate=False).astype(jnp.bfloat16)
    mlp_part = jnp.dot(act_low, full_down, preferred_element_type=jnp.float32)
    result = residual + tp_whole(mlp_part) + out_shifts[1]
    block_rows = result.astype(jnp.bfloat16)
    full_qkv, full_proj, full_up, full_down = (
        lax.all_gather(w_qkv, "fsdp", axis=1, tiled=True),
        lax.all_gather(w_proj, "fsdp", axis=1, tiled=True),
        lax.all_gather(w_up, "fsdp", axis=0, tiled=True),
        lax.all_gather(w_down, "fsdp", axis=1, tiled=True),
    )
    upstream = grad_out.reshape(row_count, width).astype(jnp.float32)
    upstream_low = upstream.astype(jnp.bfloat16)
    grad_down = contract_rows(act_low, upstream_low)
    grad_act = contract_cols(upstream_low, full_down)
    _, gelu_pull = jax.vjp(partial(jax.nn.gelu, approximate=False), pre_act)
    grad_pre = gelu_pull(grad_act)[0].astype(jnp.bfloat16)
    grad_b_up = jnp.sum(grad_pre.astype(jnp.float32), axis=0)
    grad_up = contract_rows(normed_two_low, grad_pre)
    back_part_two = contract_cols(grad_pre, full_up)
    grad_normed_two = tp_whole(back_part_two)
    _, norm_pull_two = jax.vjp(layer_norm, residual, norm_gains[1], norm_shifts[1])
    grad_res_norm, grad_gain_two, grad_shift_two = norm_pull_two(grad_normed_two)
    grad_residual = upstream + grad_res_norm
    grad_residual_low = grad_residual.astype(jnp.bfloat16)
    grad_proj = contract_rows(token_attended, grad_residual_low)
    grad_token_att = (
        contract_cols(grad_residual_low, full_proj)
        .astype(jnp.bfloat16)
        .reshape(clip_count, local_len, local_width)
    )
    grad_head_att = lax.all_to_all(grad_token_att, "ctx", split_axis=2, concat_axis=1, tiled=True)
    grad_grouped = (
        grad_head_att.reshape(clip_count, full_len, group_heads, HD)
        .transpose(0, 2, 1, 3)
        .reshape(group_count, full_len, HD)
    )
    grad_q, grad_k, grad_v = lax.map(
        backward_group, (grouped[0], grouped[1], grouped[2], grad_grouped, log_totals)
    )
    grad_heads = jnp.stack([grad_q, grad_k, grad_v]).astype(jnp.bfloat16)
    grad_heads = (
        grad_heads.reshape(3, clip_count, group_heads, full_len, HD)
        .transpose(0, 1, 3, 2, 4)
        .reshape(3, clip_count, full_len, group_heads * HD)
    )
    grad_tokens = (
        lax.all_to_all(grad_heads, "ctx", split_axis=2, concat_axis=3, tiled=True)
        .reshape(3, row_count, local_width)
        .astype(jnp.float32)
    )

    def rotate_rows(moved):
        return rotary(moved, cos_table, sin_table)

    _, rotary_pull = jax.vjp(rotate_rows, jnp.zeros(head_shape, jnp.float32))
    grad_q_pre = rotary_pull(grad_tokens[0].reshape(head_shape))[0].reshape(row_count, local_width)
    grad_k_pre = rotary_pull(grad_tokens[1].reshape(head_shape))[0].reshape(row_count, local_width)
    grad_qkv_low = jnp.stack([grad_q_pre, grad_k_pre, grad_tokens[2]]).astype(jnp.bfloat16)
    grad_b_qkv = jnp.sum(grad_qkv_low.astype(jnp.float32), axis=1)
    grad_qkv = jnp.einsum(
        "rd,cre->cde", normed_one_low, grad_qkv_low, preferred_element_type=jnp.float32
    )
    back_part_one = jnp.einsum(
        "cre,cde->rd", grad_qkv_low, full_qkv, preferred_element_type=jnp.float32
    )
    grad_normed_one = tp_whole(back_part_one)
    _, norm_pull_one = jax.vjp(layer_norm, inputs, norm_gains[0], norm_shifts[0])
    grad_in_norm, grad_gain_one, grad_shift_one = norm_pull_one(grad_normed_one)
    grad_input_rows = grad_residual + grad_in_norm
    norm_vectors = jnp.stack(
        [
            grad_gain_one,
            grad_gain_two,
            grad_shift_one,
            grad_shift_two,
            jnp.sum(grad_residual, axis=0),
            jnp.sum(upstream, axis=0),
        ]
    )
    block_output = block_rows.reshape(clip_count, local_len, width)
    grad_input = grad_input_rows.reshape(clip_count, local_len, width)
    shard_qkv, shard_proj, shard_up, shard_down = (
        lax.psum_scatter(
            grad_qkv.astype(jnp.bfloat16), "fsdp", scatter_dimension=1, tiled=True
        ).astype(jnp.float32),
        lax.psum_scatter(
            grad_proj.astype(jnp.bfloat16), "fsdp", scatter_dimension=1, tiled=True
        ).astype(jnp.float32),
        lax.psum_scatter(
            grad_up.astype(jnp.bfloat16), "fsdp", scatter_dimension=0, tiled=True
        ).astype(jnp.float32),
        lax.psum_scatter(
            grad_down.astype(jnp.bfloat16), "fsdp", scatter_dimension=1, tiled=True
        ).astype(jnp.float32),
    )
    shard_qkv, shard_proj, shard_up, shard_down = (
        lax.psum(shard_qkv.astype(jnp.bfloat16), "ctx").astype(jnp.float32),
        lax.psum(shard_proj.astype(jnp.bfloat16), "ctx").astype(jnp.float32),
        lax.psum(shard_up.astype(jnp.bfloat16), "ctx").astype(jnp.float32),
        lax.psum(shard_down.astype(jnp.bfloat16), "ctx").astype(jnp.float32),
    )
    gains_sum, shifts_sum, outs_sum, bqkv_sum, bup_sum = lax.psum(
        (norm_vectors[0:2], norm_vectors[2:4], norm_vectors[4:6], grad_b_qkv, grad_b_up),
        ("fsdp", "ctx"),
    )
    return (
        block_output,
        grad_input,
        shard_qkv,
        bqkv_sum,
        shard_proj,
        shard_up,
        bup_sum,
        shard_down,
        gains_sum,
        shifts_sum,
        outs_sum,
    )


def solution(mesh):
    in_specs = (
        P("fsdp", "ctx", None),
        P(None, "fsdp", "ctx"),
        P(None, "fsdp", "tp"),
        P(None, "tp"),
        P("tp", "fsdp"),
        P("fsdp", "tp"),
        P("tp"),
        P("tp", "fsdp"),
        P(),
        P(),
        P(),
        P("fsdp", "ctx", None),
    )
    out_specs = (
        P("fsdp", "ctx", None),
        P("fsdp", "ctx", None),
        P(None, "fsdp", "tp"),
        P(None, "tp"),
        P("tp", "fsdp"),
        P("fsdp", "tp"),
        P("tp"),
        P("tp", "fsdp"),
        P(),
        P(),
        P(),
    )
    return jax.shard_map(shards, mesh=mesh, in_specs=in_specs, out_specs=out_specs, check_vma=False)
```

profile of v0, /device:TPU:0, one launch (start us, length us, event | category | flops | bytes accessed | tf_op | source)
XLA Modules:
  0.0 875.1 jit_solution(13437522062420596701)
XLA Ops:
  7.3 2.4 copy.73
  9.7 1.9 convert_reduce_fusion.2
  15.1 2.1 fusion.40
  17.3 22.8 %all-gather.4.cloned.1.call-done = bf16[3,1024,256]{1,2,0:T(8,128)(2,1)} async-done(((bf16[3,512,256]{1,2,0:T(8,128)(2,1)}), bf16[3,1024,256]{1,2,0:T(8,128)(2,1)}) %all-gather.4.cloned.1.call-update) | async-done | bytes 1572880 | tf_op jit(solution)/shard_map/all_gather | solution.py:137
  40.1 3.9 add_bitcast_fusion
  46.6 2.1 concatenate.14
  49.0 2.1 concatenate.13
  51.5 3.1 pad_maximum_fusion.1
  54.5 3.8 all-to-all-start
  58.3 20.0 %all-to-all-done = bf16[3,2,512,256]{2,1,0,3:T(2,128)(2,1)S(1)} async-done(((bf16[3,2,512,256]{2,1,0,3:T(2,128)(2,1)}), bf16[3,2,512,256]{2,1,0,3:T(2,128)(2,1)S(1)}, u32[]{:S(2)}, u32[]{:S(2)}) %all-to-all-start) | async-done | bytes 1572896 | tf_op jit(solution)/shard_map/all_to_all | solution.py:161
  83.0 27.2 %while.54 = (s32[]{:T(128)}, bf16[2,4,512,64]{2,3,1,0:T(8,128)(2,1)}, f32[2,4,512]{2,1,0:T(4,128)S(1)}, bf16[2,2048,64]{2,1,0:T(8,128)(2,1)S(1)}, bf16[2,2048,64...) while((s32[]{:T(128)}, ...), condition=%wide.region_7.8_spmd, body=%wide.region_2.7_spmd.sunk | while | flops 277904896 | bytes 20156772 | solution.py:168
  84.4 11.4 %while.57 = (s32[]{:T(128)}, bf16[4,512,64]{1,2,0:T(8,128)(2,1)S(1)}, f32[4,512]{1,0:T(4,128)S(1)}, bf16[4,512,64]{2,1,0:T(8,128)(2,1)S(1)}, bf16[2048,64]{1,0:T...) while((s32[]{:T(128)}, bf16[4,512,64]{1,2,0:T(8,128)(2,1)S(1)}, ...), condition=%wide.region_6.6_spmd, body=%wide.region_3.5_spmd.sunk | while | flops 277904896 | bytes 13848681 | solution.py:76
  98.0 11.4 %while.57 = (s32[]{:T(128)}, bf16[4,512,64]{1,2,0:T(8,128)(2,1)S(1)}, f32[4,512]{1,0:T(4,128)S(1)}, bf16[4,512,64]{2,1,0:T(8,128)(2,1)S(1)}, bf16[2048,64]{1,0:T...) while((s32[]{:T(128)}, bf16[4,512,64]{1,2,0:T(8,128)(2,1)S(1)}, ...), condition=%wide.region_6.6_spmd, body=%wide.region_3.5_spmd.sunk | while | flops 277904896 | bytes 13848681 | solution.py:76
  110.3 2.6 copy.101
  114.4 3.5 all-to-all-start.1
  117.9 9.3 %all_gather.17 = bf16[256,1024]{1,0:T(8,128)(2,1)S(1)} all-gather(bf16[256,512]{1,0:T(8,128)(2,1)S(1)} %copy-done.30), channel_id=1, replica_groups=mesh['fsdp'=2,'ctx'=4,'tp'=4] {'fsdp'}, dimensions={1}, use_global_device_ids=true | all-gather | bytes 786432 | tf_op jit(solution)/shard_map/all_gather | solution.py:138
  128.0 1.9 copy.82
  131.1 2.1 convolution_convert_fusion.4
  135.5 84.2 %all-reduce.22.cloned.1.call-done = bf16[1024,1024]{1,0:T(8,128)(2,1)} async-done(((bf16[1024,1024]{1,0:T(8,128)(2,1)}), bf16[1024,1024]{1,0:T(8,128)(2,1)}) %all-reduce.22.cloned.1.call-update) | async-done | bytes 2097168 | tf_op jit(solution)/shard_map/psum | solution.py:55
  219.7 2.5 fusion.50
  222.2 3.0 multiply_reduce_fusion.2
  225.3 28.2 %all-gather.6.cloned.1.call-done = bf16[1024,1024]{1,0:T(8,128)(2,1)} async-done(((bf16[512,1024]{1,0:T(8,128)(2,1)}), bf16[1024,1024]{1,0:T(8,128)(2,1)}) %all-gather.6.cloned.1.call-update) | async-done | bytes 2097168 | tf_op jit(solution)/shard_map/all_gather | solution.py:139
  253.4 7.4 fusion.69
  260.8 27.1 %all-gather.8.cloned.1.call-done = bf16[1024,1024]{1,0:T(8,128)(2,1)} async-done(((bf16[1024,512]{1,0:T(8,128)(2,1)}), bf16[1024,1024]{1,0:T(8,128)(2,1)}) %all-gather.8.cloned.1.call-update) | async-done | bytes 2097168 | tf_op jit(solution)/shard_map/all_gather | solution.py:140
  287.9 16.0 %convert_reduce_fusion.4 = (f32[1024]{0:T(1024)}, bf16[1024,1024]{1,0:T(8,128)(2,1)S(1)}, f32[1024,1024]{1,0:T(8,128)}) fusion(f32[1024,1024]{1,0:T(8,128)} %fusion.69, f32[1024]{0:T(1024)S(1)} %copy-done.50, bf16[1024,1024]{1,0:T(8,128)(2,1)S(1)} %bitcast.274, bf16[1024,1024]{1,0:T(8,128)(2,1)} %all-gather.8.cloned.1.call-done), kind=kOutput, calls=%fused_computation.82 | convolution fusion | flops 2226125824 | bytes 14688256 | tf_op jit(solution)/shard_map/dot_general | solution.py:49
  305.2 3.7 convolution_convert_fusion.2
  308.9 12.1 %reduce-scatter.7.cloned.1.call-start = ((), (), s32[]{:S(2)}) async-start(), calls=%async_computation.14 | async-start | bytes 786432 | tf_op jit(solution)/shard_map/reduce_scatter | solution.py:266
  321.1 74.2 %all-reduce.24.cloned.1.call-done = bf16[1024,1024]{1,0:T(8,128)(2,1)} async-done(((bf16[1024,1024]{1,0:T(8,128)(2,1)}), bf16[1024,1024]{1,0:T(8,128)(2,1)}) %all-reduce.24.cloned.1.call-update) | async-done | bytes 2097168 | tf_op jit(solution)/shard_map/psum | solution.py:55
  395.3 4.5 convert_reduce_fusion.1
  400.0 2.7 fusion.34
  402.7 2.4 fusion.70
  405.0 2.0 copy-done.3
  408.6 4.6 multiply_convert_fusion.1
  414.5 3.8 convolution_convert_fusion
  418.3 3.0 convolution_convert_fusion.6
  422.5 3.5 all-to-all-start.2
  426.0 6.9 convolution_convert_fusion.1
  433.0 1.8 all-to-all-done.2
  436.1 103.6 %while.56 = (s32[]{:T(128)}, bf16[2,2048,64]{2,0,1:T(2,128)(2,1)}, bf16[2,2048,64]{1,2,0:T(8,128)(2,1)}, bf16[2,2048,64]{1,2,0:T(8,128)(2,1)}, bf16[2,2048,64]{2...) while((s32[]{:T(128)}, bf16[2,2048,64]{2,0,1:T(2,128)(2,1)}, ...), condition=%wide.region_19.20_spmd, body=%wide.region_15.19_spmd.sunk | while | flops 680164864 | bytes 41838996 | solution.py:217
  440.5 20.1 %while.58 = (s32[]{:T(128)}, f32[2048,64]{0,1:T(8,128)S(1)}, f32[2048,64]{0,1:T(8,128)S(1)}, f32[4,512,64]{1,2,0:T(8,128)}, bf16[4,512,64]{2,1,0:T(8,128)(2,1)S(...) while((s32[]{:T(128)}, f32[2048,64]{0,1:T(8,128)S(1)}, ...), condition=%wide.region_18.18_spmd.clone, body=%wide.region_16.17_spmd.clone.sunk | while | flops 680164864 | bytes 35530900 | solution.py:111
  462.0 25.1 %dynamic_update_slice.47 = bf16[2,2048,64]{2,0,1:T(2,128)(2,1)} dynamic-update-slice(bf16[2,2048,64]{2,0,1:T(2,128)(2,1)} %get-tuple-element.795, f32[1,2048,64]{2,0,1:T(1,128)S(1)} %bitcast.268, s32[]{:T(128)S(6)} %copy.189, s32[]{:T(128)} %constant.78.clone.1..sunk.2, s32[]{:T(128)} %constant.78.clone.1..sunk.2) | dynamic-update-slice | bytes 1048580 | tf_op jit(solution)/shard_map/while/body/jit(dynamic_update_index_in_dim)/dynamic_update_slice | solution.py:217
  492.3 20.1 %while.58 = (s32[]{:T(128)}, f32[2048,64]{0,1:T(8,128)S(1)}, f32[2048,64]{0,1:T(8,128)S(1)}, f32[4,512,64]{1,2,0:T(8,128)}, bf16[4,512,64]{2,1,0:T(8,128)(2,1)S(...) while((s32[]{:T(128)}, f32[2048,64]{0,1:T(8,128)S(1)}, ...), condition=%wide.region_18.18_spmd.clone, body=%wide.region_16.17_spmd.clone.sunk | while | flops 680164864 | bytes 35530900 | solution.py:111
  513.8 25.1 %dynamic_update_slice.47 = bf16[2,2048,64]{2,0,1:T(2,128)(2,1)} dynamic-update-slice(bf16[2,2048,64]{2,0,1:T(2,128)(2,1)} %get-tuple-element.795, f32[1,2048,64]{2,0,1:T(1,128)S(1)} %bitcast.268, s32[]{:T(128)S(6)} %copy.189, s32[]{:T(128)} %constant.78.clone.1..sunk.2, s32[]{:T(128)} %constant.78.clone.1..sunk.2) | dynamic-update-slice | bytes 1048580 | tf_op jit(solution)/shard_map/while/body/jit(dynamic_update_index_in_dim)/dynamic_update_slice | solution.py:217
  539.7 3.6 copy.142
  543.3 3.6 copy.141
  546.8 7.2 fusion.79
  554.0 3.3 reshape.228
  557.3 24.7 %all_to_all.57 = bf16[4,2,98304]{2,1,0:T(2,128)(2,1)} all-to-all(bf16[4,2,98304]{2,1,0:T(2,128)(2,1)} %reshape.228), channel_id=1, replica_groups=mesh['fsdp'=2,'ctx'=4,'tp'=4] {'ctx'}, dimensions={0} | all-to-all | bytes 3145728 | tf_op jit(solution)/shard_map/all_to_all | solution.py:227
  582.0 3.8 reshape.229
  585.8 6.4 copy.92
  601.3 4.9 fusion.61
  606.3 5.4 convolution_convert_fusion.3
  611.7 3.1 bitcast_convert_fusion
  615.2 2.1 convert_reduce_fusion.3
  618.7 11.9 %reduce-scatter.5.cloned.1.call-done = bf16[3,512,256]{1,2,0:T(8,128)(2,1)} async-done(((bf16[3,1024,256]{1,2,0:T(8,128)(2,1)}), bf16[3,512,256]{1,2,0:T(8,128)(2,1)}) %reduce-scatter.5.cloned.1.call-update) | async-done | bytes 786448 | tf_op jit(solution)/shard_map/reduce_scatter | solution.py:263
  630.7 157.9 %all-reduce.26.cloned.1.call-done = (bf16[1024,1024]{1,0:T(8,128)(2,1)}, bf16[1024,1024]{1,0:T(8,128)(2,1)}) async-done(((bf16[1024,1024]{1,0:T(8,128)(2,1)}, bf16[1024,1024]{1,0:T(8,128)(2,1)}), (bf16[1024,1024]{1,0:T(8,128)(2,1)}, bf16[1024,1024]{1,0:T(8,128)(2,1)})) %all-reduce.26.cloned.1.call-update) | async-done | bytes 4194320 | tf_op jit(solution)/shard_map/psum | solution.py:55
  788.6 3.1 convert_reduce_fusion
  791.7 2.7 fusion.35
  794.5 26.2 %all-reduce.14 = (f32[3,256]{1,0:T(4,128)}, f32[1024]{0:T(1024)}, f32[2,1024]{1,0:T(2,128)}, f32[2,1024]{1,0:T(2,128)}, f32[2,1024]{1,0:T(2,128)}) all-reduce(f32[3,256]{1,0:T(4,128)S(1)} %convert_reduce_fusion.5, f32[1024]{0:T(1024)S(1)} %copy-done.52, ...), channel_id=1, replica_groups=mesh['fsdp'=2,'ctx'=4,'tp'=4] {'fsdp','ctx'}, use_global_device_ids=true, to_apply=%region_26.27 | all-reduce | flops 7936 | bytes 63488 | tf_op jit(solution)/shard_map/psum | solution.py:282
  820.7 7.1 add_add_fusion.2
  827.9 31.4 %all-reduce.28.cloned.1.call-done = (bf16[3,512,256]{1,2,0:T(8,128)(2,1)}, bf16[256,512]{1,0:T(8,128)(2,1)}, bf16[512,1024]{1,0:T(8,128)(2,1)}, bf16[1024,512]{1,0:T(8,128)(2,1)}) async-done(((bf16[3,512,256]{1,2,0:T(8,128)(2,1)}, bf16[256,512]{1,0:T(8,128)(2,1)}, bf16[512,1024]{1,0:T(8,128)(2,1)}, bf16[1024,512]{1,0:T(8,128)(2,1)}), (bf16[3,512,256]{1,2,0:T(8,128)(2,1)}, bf16[256,512]{1,0:T(8,128)(2,1)}, ...) | async-done | bytes 3145744 | tf_op jit(solution)/shard_map/psum | solution.py:277
  859.2 1.9 convert_element_type.168
  861.1 2.5 copy.98
  863.7 2.8 convert_element_type.170
  (335 shorter events, 116.5 us)
Async XLA Ops:
  7.2 4.5 copy-start
  7.2 5.3 copy-start.46
  7.2 5.8 copy-start.47
  7.2 6.4 copy-start.48
  7.2 32.9 %all-gather.4.cloned.1.call-start = ((), (), s32[]{:S(2)}) async-start(), calls=%async_computation.8 | async-start | bytes 2359296 | tf_op jit(solution)/shard_map/all_gather | solution.py:137
  11.7 28.4 %copy-start.55 = (f32[3,256]{1,0:T(4,128)S(1)}, f32[3,256]{1,0:T(4,128)}, u32[]{:S(2)}) copy-start(f32[3,256]{1,0:T(4,128)} %param.23) | copy-start | bytes 9220
  11.7 3.4 copy-start.31
  12.5 2.6 copy-start.38
  15.0 30.8 %copy-start.15 = (f32[1024,10]{0,1:T(8,128)}, f32[1024,10]{0,1:T(8,128)S(1)}, u32[]{:S(2)}) copy-start(f32[1024,10]{0,1:T(8,128)S(1)} %get-tuple-element.436) | copy-start | bytes 122884
  15.0 30.8 %copy-start.17 = (f32[1024,10]{0,1:T(8,128)}, f32[1024,10]{0,1:T(8,128)S(1)}, u32[]{:S(2)}) copy-start(f32[1024,10]{0,1:T(8,128)S(1)} %get-tuple-element.437) | copy-start | bytes 122884
  15.0 30.8 %copy-start.19 = (f32[1024,10]{0,1:T(8,128)}, f32[1024,10]{0,1:T(8,128)S(1)}, u32[]{:S(2)}) copy-start(f32[1024,10]{0,1:T(8,128)S(1)} %get-tuple-element.438) | copy-start | bytes 122884
  15.1 30.8 %copy-start.21 = (f32[1024,10]{0,1:T(8,128)}, f32[1024,10]{0,1:T(8,128)S(1)}, u32[]{:S(2)}) copy-start(f32[1024,10]{0,1:T(8,128)S(1)} %get-tuple-element.449) | copy-start | bytes 122884
  15.1 30.8 %copy-start.23 = (f32[1024,10]{0,1:T(8,128)}, f32[1024,10]{0,1:T(8,128)S(1)}, u32[]{:S(2)}) copy-start(f32[1024,10]{0,1:T(8,128)S(1)} %get-tuple-element.450) | copy-start | bytes 122884
  15.1 30.8 %copy-start.25 = (f32[1024,10]{0,1:T(8,128)}, f32[1024,10]{0,1:T(8,128)S(1)}, u32[]{:S(2)}) copy-start(f32[1024,10]{0,1:T(8,128)S(1)} %get-tuple-element.451) | copy-start | bytes 122884
  54.5 23.8 %all-to-all-start = ((bf16[3,2,512,256]{2,1,0,3:T(2,128)(2,1)}), bf16[3,2,512,256]{2,1,0,3:T(2,128)(2,1)S(1)}, u32[]{:S(2)}, u32[]{:S(2)}) async-start(bf16[3,2,512,256]{2,1,0,3:T(2,128)(2,1)} %pad_maximum_fusion.1), calls=%async_computation | async-start | bytes 3145728 | tf_op jit(solution)/shard_map/all_to_all | solution.py:161
  84.4 11.4 %copy-start.28 = (bf16[2,4,512,64]{2,3,1,0:T(8,128)(2,1)S(1)}, bf16[2,4,512,64]{2,3,1,0:T(8,128)(2,1)}, u32[]{:S(2)}) copy-start(bf16[2,4,512,64]{2,3,1,0:T(8,128)(2,1)} %get-tuple-element.762) | copy-start | bytes 1572868 | tf_op jit(solution)/shard_map/while
  98.0 11.4 %copy-start.28 = (bf16[2,4,512,64]{2,3,1,0:T(8,128)(2,1)S(1)}, bf16[2,4,512,64]{2,3,1,0:T(8,128)(2,1)}, u32[]{:S(2)}) copy-start(bf16[2,4,512,64]{2,3,1,0:T(8,128)(2,1)} %get-tuple-element.762) | copy-start | bytes 1572868 | tf_op jit(solution)/shard_map/while
  110.2 19.6 %copy-start.5 = (bf16[2,2048,64]{2,1,0:T(8,128)(2,1)}, bf16[2,2048,64]{2,1,0:T(8,128)(2,1)S(1)}, u32[]{:S(2)}) copy-start(bf16[2,2048,64]{2,1,0:T(8,128)(2,1)S(1)} %get-tuple-element.841) | copy-start | bytes 1572868
  110.3 7.7 copy-start.30
  114.4 12.8 %all-to-all-start.1 = ((bf16[4,2,32768]{2,1,0:T(2,128)(2,1)}), bf16[4,2,32768]{2,1,0:T(2,128)(2,1)S(1)}, u32[]{:S(2)}, u32[]{:S(2)}) async-start(bf16[4,2,32768]{2,1,0:T(2,128)(2,1)} %reshape.226), calls=%async_computation.1 | async-start | bytes 1048576 | tf_op jit(solution)/shard_map/all_to_all | solution.py:174
  117.9 101.8 %all-reduce.22.cloned.1.call-start = ((), (), s32[]{:S(2)}) async-start(), calls=%async_computation.9 | async-start | bytes 4194304 | tf_op jit(solution)/shard_map/psum | solution.py:55
  129.9 5.0 copy-start.49
  129.9 89.8 %copy-start.1 = (bf16[2,512,1024]{2,1,0:T(8,128)(2,1)S(1)}, bf16[2,512,1024]{2,1,0:T(8,128)(2,1)}, u32[]{:S(2)}) copy-start(bf16[2,512,1024]{2,1,0:T(8,128)(2,1)} %param.20) | copy-start | bytes 6291460
  133.2 120.2 %all-gather.6.cloned.1.call-start = ((), (), s32[]{:S(2)}) async-start(), calls=%async_computation.10 | async-start | bytes 3145728 | tf_op jit(solution)/shard_map/all_gather | solution.py:139
  134.0 154.0 %all-gather.8.cloned.1.call-start = ((), (), s32[]{:S(2)}) async-start(), calls=%async_computation.11 | async-start | bytes 3145728 | tf_op jit(solution)/shard_map/all_gather | solution.py:140
  134.5 260.7 %all-reduce.24.cloned.1.call-start = ((), (), s32[]{:S(2)}) async-start(), calls=%async_computation.12 | async-start | bytes 4194304 | tf_op jit(solution)/shard_map/psum | solution.py:55
  135.5 89.7 %copy-start.36 = (f32[1,1024]{1,0:T(1,128)}, f32[1,1024]{1,0:T(1,128)S(1)}, u32[]{:S(2)}) copy-start(f32[1,1024]{1,0:T(1,128)S(1)} %get-tuple-element.442) | copy-start | bytes 12292
  219.7 2.5 copy-start.6
  222.2 31.2 %copy-start.35 = (f32[1,1024]{1,0:T(1,128)S(1)}, f32[1,1024]{1,0:T(1,128)}, u32[]{:S(2)}) copy-start(f32[1,1024]{1,0:T(1,128)} %get-tuple-element.443) | copy-start | bytes 12292
  222.2 31.2 %copy-start.51 = (f32[1,1024]{1,0:T(1,128)S(1)}, f32[1,1024]{1,0:T(1,128)}, u32[]{:S(2)}) copy-start(f32[1,1024]{1,0:T(1,128)} %get-tuple-element.445) | copy-start | bytes 12292
  253.4 34.5 %copy-start.10 = (bf16[2,512,1024]{2,1,0:T(8,128)(2,1)S(1)}, bf16[2,512,1024]{2,1,0:T(8,128)(2,1)}, u32[]{:S(2)}) copy-start(bf16[2,512,1024]{2,1,0:T(8,128)(2,1)} %param.31) | copy-start | bytes 6291460
  253.4 34.5 %copy-start.50 = (f32[1024]{0:T(1024)S(1)}, f32[1024]{0:T(1024)}, u32[]{:S(2)}) copy-start(f32[1024]{0:T(1024)} %param.26) | copy-start | bytes 12292
  287.9 17.3 %copy-start.53 = (bf16[1024,1024]{1,0:T(8,128)(2,1)S(1)}, bf16[1024,1024]{1,0:T(8,128)(2,1)}, u32[]{:S(2)}) copy-start(bf16[1024,1024]{1,0:T(8,128)(2,1)} %all-gather.6.cloned.1.call-done) | copy-start | bytes 6291460
  308.9 309.7 %reduce-scatter.7.cloned.1.call-start = ((), (), s32[]{:S(2)}) async-start(), calls=%async_computation.14 | async-start | bytes 786432 | tf_op jit(solution)/shard_map/reduce_scatter | solution.py:266
  395.2 4.5 copy-start.4
  395.3 4.7 copy-start.7
  405.0 2.0 copy-start.3
  408.5 210.2 %reduce-scatter.11.cloned.1.call-start = ((), (), s32[]{:S(2)}) async-start(), calls=%async_computation.16 | async-start | bytes 3145728 | tf_op jit(solution)/shard_map/reduce_scatter | solution.py:272
  422.5 12.3 %all-to-all-start.2 = ((bf16[2,512,256]{1,0,2:T(2,128)(2,1)}), bf16[2,512,256]{1,0,2:T(2,128)(2,1)S(1)}, u32[]{:S(2)}, u32[]{:S(2)}) async-start(bf16[2,512,256]{1,0,2:T(2,128)(2,1)} %copy.83), calls=%async_computation.2 | async-start | bytes 1048576 | tf_op jit(solution)/shard_map/all_to_all | solution.py:211
  426.0 192.7 %reduce-scatter.9.cloned.1.call-start = ((), (), s32[]{:S(2)}) async-start(), calls=%async_computation.15 | async-start | bytes 3145728 | tf_op jit(solution)/shard_map/reduce_scatter | solution.py:269
  432.9 197.7 %reduce-scatter.5.cloned.1.call-start = ((), (), s32[]{:S(2)}) async-start(), calls=%async_computation.13 | async-start | bytes 2359296 | tf_op jit(solution)/shard_map/reduce_scatter | solution.py:263
  592.2 2.9 copy-start.9
  596.4 1.7 copy-start.16
  596.4 1.7 copy-start.18
  596.4 1.7 copy-start.20
  598.9 2.4 copy-start.13
  601.3 5.0 copy-start.12
  606.2 182.3 %all-reduce.26.cloned.1.call-start = ((), (), s32[]{:S(2)}) async-start(), calls=%async_computation.17 | async-start | bytes 8388608 | tf_op jit(solution)/shard_map/psum | solution.py:55
  606.3 5.4 copy-start.14
  606.3 5.4 copy-start.54
  614.8 2.5 copy-start.42
  614.8 173.7 %copy-start.2 = (bf16[2,512,1024]{2,1,0:T(8,128)(2,1)S(1)}, bf16[2,512,1024]{2,1,0:T(8,128)(2,1)}, u32[]{:S(2)}) copy-start(bf16[2,512,1024]{2,1,0:T(8,128)(2,1)} %param.20) | copy-start | bytes 6291460
  614.8 173.7 %copy-start.32 = (f32[1,4,2,128]{3,1,2,0:T(4,128)S(1)}, f32[1,4,2,128]{3,1,2,0:T(4,128)}, u32[]{:S(2)}) copy-start(f32[1,4,2,128]{3,1,2,0:T(4,128)} %copy-done.31) | copy-start | bytes 12292
  614.9 173.7 %copy-start.34 = (f32[1,1024]{1,0:T(1,128)S(1)}, f32[1,1024]{1,0:T(1,128)}, u32[]{:S(2)}) copy-start(f32[1,1024]{1,0:T(1,128)} %copy-done.33) | copy-start | bytes 12292
  614.9 244.4 %all-reduce.28.cloned.1.call-start = ((), (), s32[]{:S(2)}) async-start(), calls=%async_computation.18 | async-start | bytes 6291456 | tf_op jit(solution)/shard_map/psum | solution.py:277
  617.3 174.4 %copy-start.41 = (f32[1,4,2,128]{3,1,2,0:T(4,128)S(1)}, f32[1,4,2,128]{3,1,2,0:T(4,128)}, u32[]{:S(2)}) copy-start(f32[1,4,2,128]{3,1,2,0:T(4,128)} %copy-done.40) | copy-start | bytes 12292
  617.3 174.4 %copy-start.44 = (f32[1024]{0:T(1024)S(1)}, f32[1024]{0:T(1024)}, u32[]{:S(2)}) copy-start(f32[1024]{0:T(1024)} %get-tuple-element.296) | copy-start | bytes 12292
  617.3 174.4 %copy-start.39 = (f32[1024]{0:T(1024)S(1)}, f32[1024]{0:T(1024)}, u32[]{:S(2)}) copy-start(f32[1024]{0:T(1024)} %copy-done.38) | copy-start | bytes 12292
  788.5 3.2 copy-start.8
  788.5 5.9 copy-start.43
  788.5 5.9 copy-start.52
  788.6 32.2 %copy-start.37 = (f32[1,1024]{1,0:T(1,128)S(1)}, f32[1,1024]{1,0:T(1,128)}, u32[]{:S(2)}) copy-start(f32[1,1024]{1,0:T(1,128)} %copy-done.36) | copy-start | bytes 12292
  788.6 32.2 %copy-start.45 = (f32[1,1024]{1,0:T(1,128)S(1)}, f32[1,1024]{1,0:T(1,128)}, u32[]{:S(2)}) copy-start(f32[1,1024]{1,0:T(1,128)} %get-tuple-element.441) | copy-start | bytes 12292
  859.2 7.2 copy-start.27
  (9 other events, 11.5 us)
Sparse Core Ops, SparseCore 0:
  10.1 29.8 all-gather.3
  133.3 86.3 all-reduce.21
  221.2 32.1 all-gather.5
  254.8 33.0 all-gather.7
  309.1 86.1 all-reduce.23
  408.7 13.6 reduce-scatter.6
  424.6 31.8 reduce-scatter.10
  458.8 31.8 reduce-scatter.8
  606.3 24.2 reduce-scatter.4
  633.5 155.0 all-reduce.25
  791.1 68.0 all-reduce.27
where the time goes:
time: 888 us; the launch traced here: 875 us
  waiting for transfers between devices  461 us (52%)
  local copies, waits for them, and re-layouts  130 us (15%)
  matrix products  113 us (13%)
  other arithmetic  71.1 us (8%)
  blocking collectives  60.2 us (7%)
  starting transfers between devices  23.8 us (3%)
  between operations  15.3 us (2%)
    psum x3, waiting for transfers between devices, tp_whole(): return lax.psum(partial_sum.astype(jnp.bfloat16), 'tp').astype(jnp.float32)  316 us
    dynamic_update_slice x4, local copies, waits for them, and re-layouts, shards(): lax.map(backward_group, (grouped[0], grouped[1], grouped[2], grad_grouped...  51.9 us
    psum x1, waiting for transfers between devices, shards(): lax.psum(shard_qkv.astype(jnp.bfloat16), 'ctx').astype(jnp.float32)  31.4 us
    unnamed x122, local copies, waits for them, and re-layouts  28.2 us
    all_gather x1, waiting for transfers between devices, shards(): lax.all_gather(w_up, 'fsdp', axis=0, tiled=True)  28.2 us
    all_gather x1, waiting for transfers between devices, shards(): lax.all_gather(w_down, 'fsdp', axis=1, tiled=True)  27.1 us
    psum x1, blocking collectives, shards(): lax.psum((norm_vectors[0:2], norm_vectors[2:4], norm_vectors[4:6], grad_b...  26.2 us
    all_to_all x1, blocking collectives, shards(): lax.all_to_all(grad_heads, 'ctx', split_axis=2, concat_axis=3, tiled=True)  24.7 us
  transfers between devices with their start and end apart: 14, of which 10 were waited for; matrix products, arithmetic and copies ran while one was open for 24% of the time, Pallas kernels for 0%

commit v1 on v0

--- a/solution.py
+++ b/solution.py
@@ -224,7 +224,12 @@
         .reshape(3, clip_count, full_len, group_heads * HD)
     )
     grad_tokens = (
-        lax.all_to_all(grad_heads, "ctx", split_axis=2, concat_axis=3, tiled=True)
+        jnp.concatenate(
+            lax.all_to_all(
+                jnp.stack(jnp.split(grad_heads, lax.axis_size("ctx"), axis=2)), "ctx", 0, 0
+            ),
+            axis=3,
+        )
         .reshape(3, row_count, local_width)
         .astype(jnp.float32)
     )

time: 888 us -> 805 us (0.907)
  local copies, waits for them, and re-layouts: 130 us -> 64 us
    dynamic_update_slice x4 -> x6, local copies, waits for them, and re-layouts: 51.9 us -> 3.59 us  [shards(): lax.map(backward_group, (grouped[0], grouped[1], grouped[2], grad_grouped...]
    unnamed x122, local copies, waits for them, and re-layouts: 28.2 us -> 14.8 us
  transfers between devices with their start and end apart: 14 -> 14, of which waited for: 10 -> 10; matrix products, arithmetic and copies ran while one was open for 24% -> 16% of each run, Pallas kernels for 0% -> 0%
where the time goes in v1:
time: 805 us; the launch traced here: 797 us
  waiting for transfers between devices  462 us (57%)
  matrix products  110 us (14%)
  other arithmetic  64.8 us (8%)
  local copies, waits for them, and re-layouts  64 us (8%)
  blocking collectives  58.3 us (7%)
  starting transfers between devices  22.7 us (3%)
  between operations  15.3 us (2%)
    psum x3, waiting for transfers between devices, tp_whole(): return lax.psum(partial_sum.astype(jnp.bfloat16), 'tp').astype(jnp.float32)  317 us
    psum x1, waiting for transfers between devices, shards(): lax.psum(shard_qkv.astype(jnp.bfloat16), 'ctx').astype(jnp.float32)  31.4 us
    all_gather x1, waiting for transfers between devices, shards(): lax.all_gather(w_up, 'fsdp', axis=0, tiled=True)  28.2 us
    all_gather x1, waiting for transfers between devices, shards(): lax.all_gather(w_down, 'fsdp', axis=1, tiled=True)  27.1 us
    psum x1, blocking collectives, shards(): lax.psum((norm_vectors[0:2], norm_vectors[2:4], norm_vectors[4:6], grad_b...  26.2 us
    all_gather x1, waiting for transfers between devices, shards(): lax.all_gather(w_qkv, 'fsdp', axis=1, tiled=True)  22.9 us
    dot_general x3, matrix products, contract_cols(): lax.dot_general(left_mat, right_mat, (((1,), (1,)), ((), ())), preferred_...  22.7 us
    all_to_all x1, blocking collectives, shards(): lax.all_to_all(jnp.stack(jnp.split(grad_heads, lax.axis_size('ctx'), axis...  22.7 us
  transfers between devices with their start and end apart: 14, of which 10 were waited for; matrix products, arithmetic and copies ran while one was open for 16% of the time, Pallas kernels for 0%

profile of v1, /device:TPU:0, one launch (start us, length us, event | category | flops | bytes accessed | tf_op | source)
XLA Modules:
  0.0 797.4 jit_solution(14894585414075408104)
XLA Ops:
  7.3 2.4 copy.75
  9.7 1.9 convert_reduce_fusion.2
  15.1 2.1 fusion.40
  17.2 22.9 %all-gather.4.cloned.1.call-done = bf16[3,1024,256]{1,2,0:T(8,128)(2,1)} async-done(((bf16[3,512,256]{1,2,0:T(8,128)(2,1)}), bf16[3,1024,256]{1,2,0:T(8,128)(2,1)}) %all-gather.4.cloned.1.call-update) | async-done | bytes 1572880 | tf_op jit(solution)/shard_map/all_gather | solution.py:137
  40.1 3.9 add_bitcast_fusion
  46.5 2.1 concatenate.14
  49.0 2.1 concatenate.13
  51.4 3.1 pad_maximum_fusion
  54.5 3.8 all-to-all-start
  58.3 20.0 %all-to-all-done = bf16[3,2,512,256]{2,1,0,3:T(2,128)(2,1)S(1)} async-done(((bf16[3,2,512,256]{2,1,0,3:T(2,128)(2,1)}), bf16[3,2,512,256]{2,1,0,3:T(2,128)(2,1)S(1)}, u32[]{:S(2)}, u32[]{:S(2)}) %all-to-all-start) | async-done | bytes 1572896 | tf_op jit(solution)/shard_map/all_to_all | solution.py:161
  78.3 2.3 fusion.75
  80.6 1.6 copy.81
  82.2 2.2 copy.80
  85.7 28.9 %while.54 = (s32[]{:T(128)}, bf16[2,4,512,64]{2,3,1,0:T(8,128)(2,1)}, f32[2,4,512]{2,1,0:T(4,128)S(1)}, bf16[2,2048,64]{2,1,0:T(8,128)(2,1)}, bf16[2,2048,64]{2,...) while((s32[]{:T(128)}, ...), condition=%wide.region_7.8_spmd, body=%wide.region_2.7_spmd.sunk | while | flops 277904896 | bytes 20156772 | solution.py:168
  87.9 11.4 %while.57 = (s32[]{:T(128)}, bf16[4,512,64]{1,2,0:T(8,128)(2,1)S(1)}, f32[4,512]{1,0:T(4,128)S(1)}, bf16[4,512,64]{2,1,0:T(8,128)(2,1)S(1)}, bf16[2048,64]{1,0:T...) while((s32[]{:T(128)}, bf16[4,512,64]{1,2,0:T(8,128)(2,1)S(1)}, ...), condition=%wide.region_6.6_spmd, body=%wide.region_3.5_spmd.sunk | while | flops 277904896 | bytes 13848681 | solution.py:76
  102.4 11.4 %while.57 = (s32[]{:T(128)}, bf16[4,512,64]{1,2,0:T(8,128)(2,1)S(1)}, f32[4,512]{1,0:T(4,128)S(1)}, bf16[4,512,64]{2,1,0:T(8,128)(2,1)S(1)}, bf16[2048,64]{1,0:T...) while((s32[]{:T(128)}, bf16[4,512,64]{1,2,0:T(8,128)(2,1)S(1)}, ...), condition=%wide.region_6.6_spmd, body=%wide.region_3.5_spmd.sunk | while | flops 277904896 | bytes 13848681 | solution.py:76
  114.7 2.4 copy.103
  117.1 1.6 reshape.224
  118.6 3.5 all-to-all-start.1
  122.2 9.4 %all_gather.17 = bf16[256,1024]{1,0:T(8,128)(2,1)} all-gather(bf16[256,512]{1,0:T(8,128)(2,1)S(1)} %copy-done.34), channel_id=1, replica_groups=mesh['fsdp'=2,'ctx'=4,'tp'=4] {'fsdp'}, dimensions={1}, use_global_device_ids=true | all-gather | bytes 786432 | tf_op jit(solution)/shard_map/all_gather | solution.py:138
  132.3 1.9 copy.84
  136.3 3.1 convolution_convert_fusion.4
  141.7 84.2 %all-reduce.22.cloned.1.call-done = bf16[1024,1024]{1,0:T(8,128)(2,1)} async-done(((bf16[1024,1024]{1,0:T(8,128)(2,1)}), bf16[1024,1024]{1,0:T(8,128)(2,1)}) %all-reduce.22.cloned.1.call-update) | async-done | bytes 2097168 | tf_op jit(solution)/shard_map/psum | solution.py:55
  225.8 2.5 fusion.50
  228.4 3.0 multiply_reduce_fusion.2
  231.4 28.2 %all-gather.6.cloned.1.call-done = bf16[1024,1024]{1,0:T(8,128)(2,1)} async-done(((bf16[512,1024]{1,0:T(8,128)(2,1)}), bf16[1024,1024]{1,0:T(8,128)(2,1)}) %all-gather.6.cloned.1.call-update) | async-done | bytes 2097168 | tf_op jit(solution)/shard_map/all_gather | solution.py:139
  259.6 7.4 fusion.69
  267.0 27.1 %all-gather.8.cloned.1.call-done = bf16[1024,1024]{1,0:T(8,128)(2,1)} async-done(((bf16[1024,512]{1,0:T(8,128)(2,1)}), bf16[1024,1024]{1,0:T(8,128)(2,1)}) %all-gather.8.cloned.1.call-update) | async-done | bytes 2097168 | tf_op jit(solution)/shard_map/all_gather | solution.py:140
  294.1 15.9 %convert_reduce_fusion.4 = (f32[1024]{0:T(1024)}, bf16[1024,1024]{1,0:T(8,128)(2,1)S(1)}, f32[1024,1024]{1,0:T(8,128)}) fusion(f32[1024,1024]{1,0:T(8,128)} %fusion.69, f32[1024]{0:T(1024)S(1)} %copy-done.54, bf16[1024,1024]{1,0:T(8,128)(2,1)S(1)} %bitcast.276, bf16[1024,1024]{1,0:T(8,128)(2,1)} %all-gather.8.cloned.1.call-done), kind=kOutput, calls=%fused_computation.83 | convolution fusion | flops 2226125824 | bytes 14688256 | tf_op jit(solution)/shard_map/dot_general | solution.py:49
  311.4 3.7 convolution_convert_fusion.2
  315.1 11.0 %reduce-scatter.7.cloned.1.call-start = ((), (), s32[]{:S(2)}) async-start(), calls=%async_computation.14 | async-start | bytes 786432 | tf_op jit(solution)/shard_map/reduce_scatter | solution.py:271
  326.1 75.3 %all-reduce.24.cloned.1.call-done = bf16[1024,1024]{1,0:T(8,128)(2,1)} async-done(((bf16[1024,1024]{1,0:T(8,128)(2,1)}), bf16[1024,1024]{1,0:T(8,128)(2,1)}) %all-reduce.24.cloned.1.call-update) | async-done | bytes 2097168 | tf_op jit(solution)/shard_map/psum | solution.py:55
  401.4 4.5 convert_reduce_fusion.1
  406.1 2.7 fusion.34
  408.8 2.4 fusion.70
  411.2 2.0 copy-done.3
  413.1 1.6 convolution_convert_fusion.5
  414.8 4.6 multiply_convert_fusion.1
  420.7 3.8 convolution_convert_fusion
  424.5 3.1 convolution_convert_fusion.6
  428.8 3.5 all-to-all-start.2
  432.3 6.9 convolution_convert_fusion.1
  439.3 1.8 all-to-all-done.2
  442.4 47.7 %while.56 = (s32[]{:T(128)}, bf16[2,2048,64]{1,2,0:T(8,128)(2,1)}, bf16[2,2048,64]{1,2,0:T(8,128)(2,1)}, bf16[2,2048,64]{1,2,0:T(8,128)(2,1)}, bf16[2,2048,64]{2...) while((s32[]{:T(128)}, bf16[2,2048,64]{1,2,0:T(8,128)(2,1)}, ...), condition=%wide.region_19.20_spmd, body=%wide.region_15.19_spmd.sunk | while | flops 680164864 | bytes 45771212 | solution.py:217
  446.7 17.5 %while.58 = (s32[]{:T(128)}, f32[2048,64]{0,1:T(8,128)S(1)}, f32[2048,64]{0,1:T(8,128)S(1)}, bf16[4,512,64]{1,2,0:T(8,128)(2,1)S(1)}, bf16[4,512,64]{2,1,0:T(8,1...) while((s32[]{:T(128)}, f32[2048,64]{0,1:T(8,128)S(1)}, ...), condition=%wide.region_18.18_spmd.clone, body=%wide.region_16.17_spmd.clone.sunk | while | flops 680164864 | bytes 35793044 | solution.py:111
  470.6 17.5 %while.58 = (s32[]{:T(128)}, f32[2048,64]{0,1:T(8,128)S(1)}, f32[2048,64]{0,1:T(8,128)S(1)}, bf16[4,512,64]{1,2,0:T(8,128)(2,1)S(1)}, bf16[4,512,64]{2,1,0:T(8,1...) while((s32[]{:T(128)}, f32[2048,64]{0,1:T(8,128)S(1)}, ...), condition=%wide.region_18.18_spmd.clone, body=%wide.region_16.17_spmd.clone.sunk | while | flops 680164864 | bytes 35793044 | solution.py:111
  490.2 1.5 pad_maximum_fusion.1
  492.0 22.7 %all_to_all.53 = bf16[4,3,2,512,64]{3,4,2,1,0:T(8,128)(2,1)S(1)} all-to-all(bf16[4,3,2,512,64]{3,4,2,1,0:T(8,128)(2,1)S(1)} %pad_maximum_fusion.2), channel_id=1, replica_groups=mesh['fsdp'=2,'ctx'=4,'tp'=4] {'ctx'}, dimensions={0} | all-to-all | bytes 3145728 | tf_op jit(solution)/shard_map/all_to_all | solution.py:228
  515.5 1.5 reshape.223
  523.4 5.1 fusion.61
  528.7 5.4 convolution_convert_fusion.3
  534.1 3.1 bitcast_convert_fusion
  537.6 2.1 convert_reduce_fusion.3
  541.1 11.8 %reduce-scatter.5.cloned.1.call-done = bf16[3,512,256]{1,2,0:T(8,128)(2,1)} async-done(((bf16[3,1024,256]{1,2,0:T(8,128)(2,1)}), bf16[3,512,256]{1,2,0:T(8,128)(2,1)}) %reduce-scatter.5.cloned.1.call-update) | async-done | bytes 786448 | tf_op jit(solution)/shard_map/reduce_scatter | solution.py:268
  553.0 157.9 %all-reduce.26.cloned.1.call-done = (bf16[1024,1024]{1,0:T(8,128)(2,1)}, bf16[1024,1024]{1,0:T(8,128)(2,1)}) async-done(((bf16[1024,1024]{1,0:T(8,128)(2,1)}, bf16[1024,1024]{1,0:T(8,128)(2,1)}), (bf16[1024,1024]{1,0:T(8,128)(2,1)}, bf16[1024,1024]{1,0:T(8,128)(2,1)})) %all-reduce.26.cloned.1.call-update) | async-done | bytes 4194320 | tf_op jit(solution)/shard_map/psum | solution.py:55
  710.9 3.1 convert_reduce_fusion
  714.1 2.7 fusion.35
  716.8 26.2 %all-reduce.14 = (f32[3,256]{1,0:T(4,128)}, f32[1024]{0:T(1024)}, f32[2,1024]{1,0:T(2,128)}, f32[2,1024]{1,0:T(2,128)}, f32[2,1024]{1,0:T(2,128)}) all-reduce(f32[3,256]{1,0:T(4,128)S(1)} %convert_reduce_fusion.5, f32[1024]{0:T(1024)S(1)} %copy-done.56, ...), channel_id=1, replica_groups=mesh['fsdp'=2,'ctx'=4,'tp'=4] {'fsdp','ctx'}, use_global_device_ids=true, to_apply=%region_26.27 | all-reduce | flops 7936 | bytes 63488 | tf_op jit(solution)/shard_map/psum | solution.py:287
  743.1 7.1 add_add_fusion.2
  750.2 31.4 %all-reduce.28.cloned.1.call-done = (bf16[3,512,256]{1,2,0:T(8,128)(2,1)}, bf16[256,512]{1,0:T(8,128)(2,1)}, bf16[512,1024]{1,0:T(8,128)(2,1)}, bf16[1024,512]{1,0:T(8,128)(2,1)}) async-done(((bf16[3,512,256]{1,2,0:T(8,128)(2,1)}, bf16[256,512]{1,0:T(8,128)(2,1)}, bf16[512,1024]{1,0:T(8,128)(2,1)}, bf16[1024,512]{1,0:T(8,128)(2,1)}), (bf16[3,512,256]{1,2,0:T(8,128)(2,1)}, bf16[256,512]{1,0:T(8,128)(2,1)}, ...) | async-done | bytes 3145744 | tf_op jit(solution)/shard_map/psum | solution.py:282
  781.6 1.9 convert_element_type.164
  783.5 2.5 copy.100
  786.0 2.8 convert_element_type.166
  788.8 1.6 convert_element_type.169
  (348 shorter events, 103.5 us)
Async XLA Ops:
  7.2 4.5 copy-start
  7.2 5.3 copy-start.50
  7.2 5.8 copy-start.51
  7.2 6.4 copy-start.52
  7.2 32.9 %all-gather.4.cloned.1.call-start = ((), (), s32[]{:S(2)}) async-start(), calls=%async_computation.8 | async-start | bytes 2359296 | tf_op jit(solution)/shard_map/all_gather | solution.py:137
  11.7 28.4 %copy-start.59 = (f32[3,256]{1,0:T(4,128)S(1)}, f32[3,256]{1,0:T(4,128)}, u32[]{:S(2)}) copy-start(f32[3,256]{1,0:T(4,128)} %param.23) | copy-start | bytes 9220
  11.7 32.3 %copy-start.35 = (f32[1,4,2,128]{3,1,2,0:T(4,128)}, f32[1,4,2,128]{3,1,2,0:T(4,128)S(1)}, u32[]{:S(2)}) copy-start(f32[1,4,2,128]{3,1,2,0:T(4,128)S(1)} %copy.141) | copy-start | bytes 12292
  12.5 31.5 %copy-start.42 = (f32[1024]{0:T(1024)}, f32[1024]{0:T(1024)S(1)}, u32[]{:S(2)}) copy-start(f32[1024]{0:T(1024)S(1)} %rsqrt.22) | copy-start | bytes 12292
  13.6 30.3 %copy-start.37 = (f32[1,1024]{1,0:T(1,128)}, f32[1,1024]{1,0:T(1,128)S(1)}, u32[]{:S(2)}) copy-start(f32[1,1024]{1,0:T(1,128)S(1)} %get-tuple-element.448) | copy-start | bytes 12292
  15.0 30.8 %copy-start.19 = (f32[1024,10]{0,1:T(8,128)}, f32[1024,10]{0,1:T(8,128)S(1)}, u32[]{:S(2)}) copy-start(f32[1024,10]{0,1:T(8,128)S(1)} %get-tuple-element.440) | copy-start | bytes 122884
  15.0 30.8 %copy-start.21 = (f32[1024,10]{0,1:T(8,128)}, f32[1024,10]{0,1:T(8,128)S(1)}, u32[]{:S(2)}) copy-start(f32[1024,10]{0,1:T(8,128)S(1)} %get-tuple-element.441) | copy-start | bytes 122884
  15.1 30.8 %copy-start.23 = (f32[1024,10]{0,1:T(8,128)}, f32[1024,10]{0,1:T(8,128)S(1)}, u32[]{:S(2)}) copy-start(f32[1024,10]{0,1:T(8,128)S(1)} %get-tuple-element.442) | copy-start | bytes 122884
  15.1 30.8 %copy-start.25 = (f32[1024,10]{0,1:T(8,128)}, f32[1024,10]{0,1:T(8,128)S(1)}, u32[]{:S(2)}) copy-start(f32[1024,10]{0,1:T(8,128)S(1)} %get-tuple-element.453) | copy-start | bytes 122884
  15.1 30.8 %copy-start.27 = (f32[1024,10]{0,1:T(8,128)}, f32[1024,10]{0,1:T(8,128)S(1)}, u32[]{:S(2)}) copy-start(f32[1024,10]{0,1:T(8,128)S(1)} %get-tuple-element.454) | copy-start | bytes 122884
  15.1 30.8 %copy-start.29 = (f32[1024,10]{0,1:T(8,128)}, f32[1024,10]{0,1:T(8,128)S(1)}, u32[]{:S(2)}) copy-start(f32[1024,10]{0,1:T(8,128)S(1)} %get-tuple-element.455) | copy-start | bytes 122884
  54.5 23.8 %all-to-all-start = ((bf16[3,2,512,256]{2,1,0,3:T(2,128)(2,1)}), bf16[3,2,512,256]{2,1,0,3:T(2,128)(2,1)S(1)}, u32[]{:S(2)}, u32[]{:S(2)}) async-start(bf16[3,2,512,256]{2,1,0,3:T(2,128)(2,1)} %pad_maximum_fusion), calls=%async_computation | async-start | bytes 3145728 | tf_op jit(solution)/shard_map/all_to_all | solution.py:161
  87.9 11.4 %copy-start.32 = (bf16[2,4,512,64]{2,3,1,0:T(8,128)(2,1)S(1)}, bf16[2,4,512,64]{2,3,1,0:T(8,128)(2,1)}, u32[]{:S(2)}) copy-start(bf16[2,4,512,64]{2,3,1,0:T(8,128)(2,1)} %get-tuple-element.766) | copy-start | bytes 1572868 | tf_op jit(solution)/shard_map/while
  102.4 11.4 %copy-start.32 = (bf16[2,4,512,64]{2,3,1,0:T(8,128)(2,1)S(1)}, bf16[2,4,512,64]{2,3,1,0:T(8,128)(2,1)}, u32[]{:S(2)}) copy-start(bf16[2,4,512,64]{2,3,1,0:T(8,128)(2,1)} %get-tuple-element.766) | copy-start | bytes 1572868 | tf_op jit(solution)/shard_map/while
  114.7 7.5 copy-start.34
  118.6 12.9 %all-to-all-start.1 = ((bf16[4,2,32768]{2,1,0:T(2,128)(2,1)}), bf16[4,2,32768]{2,1,0:T(2,128)(2,1)S(1)}, u32[]{:S(2)}, u32[]{:S(2)}) async-start(bf16[4,2,32768]{2,1,0:T(2,128)(2,1)} %reshape.224), calls=%async_computation.1 | async-start | bytes 1048576 | tf_op jit(solution)/shard_map/all_to_all | solution.py:174
  122.1 103.7 %all-reduce.22.cloned.1.call-start = ((), (), s32[]{:S(2)}) async-start(), calls=%async_computation.9 | async-start | bytes 4194304 | tf_op jit(solution)/shard_map/psum | solution.py:55
  134.2 6.9 copy-start.53
  134.2 91.6 %copy-start.1 = (bf16[2,512,1024]{2,1,0:T(8,128)(2,1)S(1)}, bf16[2,512,1024]{2,1,0:T(8,128)(2,1)}, u32[]{:S(2)}) copy-start(bf16[2,512,1024]{2,1,0:T(8,128)(2,1)} %param.20) | copy-start | bytes 6291460
  139.4 120.2 %all-gather.6.cloned.1.call-start = ((), (), s32[]{:S(2)}) async-start(), calls=%async_computation.10 | async-start | bytes 3145728 | tf_op jit(solution)/shard_map/all_gather | solution.py:139
  140.1 153.9 %all-gather.8.cloned.1.call-start = ((), (), s32[]{:S(2)}) async-start(), calls=%async_computation.11 | async-start | bytes 3145728 | tf_op jit(solution)/shard_map/all_gather | solution.py:140
  140.7 260.7 %all-reduce.24.cloned.1.call-start = ((), (), s32[]{:S(2)}) async-start(), calls=%async_computation.12 | async-start | bytes 4194304 | tf_op jit(solution)/shard_map/psum | solution.py:55
  141.7 89.7 %copy-start.40 = (f32[1,1024]{1,0:T(1,128)}, f32[1,1024]{1,0:T(1,128)S(1)}, u32[]{:S(2)}) copy-start(f32[1,1024]{1,0:T(1,128)S(1)} %get-tuple-element.446) | copy-start | bytes 12292
  225.8 2.5 copy-start.7
  228.4 31.2 %copy-start.39 = (f32[1,1024]{1,0:T(1,128)S(1)}, f32[1,1024]{1,0:T(1,128)}, u32[]{:S(2)}) copy-start(f32[1,1024]{1,0:T(1,128)} %get-tuple-element.447) | copy-start | bytes 12292
  228.4 31.2 %copy-start.55 = (f32[1,1024]{1,0:T(1,128)S(1)}, f32[1,1024]{1,0:T(1,128)}, u32[]{:S(2)}) copy-start(f32[1,1024]{1,0:T(1,128)} %get-tuple-element.449) | copy-start | bytes 12292
  259.6 34.5 %copy-start.10 = (bf16[2,512,1024]{2,1,0:T(8,128)(2,1)S(1)}, bf16[2,512,1024]{2,1,0:T(8,128)(2,1)}, u32[]{:S(2)}) copy-start(bf16[2,512,1024]{2,1,0:T(8,128)(2,1)} %param.31) | copy-start | bytes 6291460
  259.6 34.5 %copy-start.54 = (f32[1024]{0:T(1024)S(1)}, f32[1024]{0:T(1024)}, u32[]{:S(2)}) copy-start(f32[1024]{0:T(1024)} %param.26) | copy-start | bytes 12292
  294.1 17.3 %copy-start.57 = (bf16[1024,1024]{1,0:T(8,128)(2,1)S(1)}, bf16[1024,1024]{1,0:T(8,128)(2,1)}, u32[]{:S(2)}) copy-start(bf16[1024,1024]{1,0:T(8,128)(2,1)} %all-gather.6.cloned.1.call-done) | copy-start | bytes 6291460
  315.1 226.0 %reduce-scatter.7.cloned.1.call-start = ((), (), s32[]{:S(2)}) async-start(), calls=%async_computation.14 | async-start | bytes 786432 | tf_op jit(solution)/shard_map/reduce_scatter | solution.py:271
  401.4 4.5 copy-start.4
  401.4 4.7 copy-start.8
  408.8 4.3 copy-start.12
  414.7 126.4 %reduce-scatter.11.cloned.1.call-start = ((), (), s32[]{:S(2)}) async-start(), calls=%async_computation.16 | async-start | bytes 3145728 | tf_op jit(solution)/shard_map/reduce_scatter | solution.py:277
  428.8 12.3 %all-to-all-start.2 = ((bf16[2,512,256]{1,0,2:T(2,128)(2,1)}), bf16[2,512,256]{1,0,2:T(2,128)(2,1)S(1)}, u32[]{:S(2)}, u32[]{:S(2)}) async-start(bf16[2,512,256]{1,0,2:T(2,128)(2,1)} %copy.85), calls=%async_computation.2 | async-start | bytes 1048576 | tf_op jit(solution)/shard_map/all_to_all | solution.py:211
  432.3 108.8 %reduce-scatter.9.cloned.1.call-start = ((), (), s32[]{:S(2)}) async-start(), calls=%async_computation.15 | async-start | bytes 3145728 | tf_op jit(solution)/shard_map/reduce_scatter | solution.py:274
  439.2 113.7 %reduce-scatter.5.cloned.1.call-start = ((), (), s32[]{:S(2)}) async-start(), calls=%async_computation.13 | async-start | bytes 2359296 | tf_op jit(solution)/shard_map/reduce_scatter | solution.py:268
  464.2 2.1 copy-start.6
  488.1 2.1 copy-start.6
  523.4 5.2 copy-start.17
  523.4 5.2 copy-start.14
  528.5 5.5 copy-start.15
  528.6 5.5 copy-start.16
  528.6 182.3 %all-reduce.26.cloned.1.call-start = ((), (), s32[]{:S(2)}) async-start(), calls=%async_computation.17 | async-start | bytes 8388608 | tf_op jit(solution)/shard_map/psum | solution.py:55
  528.6 5.4 copy-start.18
  528.6 5.4 copy-start.58
  537.2 2.5 copy-start.46
  537.2 173.6 %copy-start.2 = (bf16[2,512,1024]{2,1,0:T(8,128)(2,1)S(1)}, bf16[2,512,1024]{2,1,0:T(8,128)(2,1)}, u32[]{:S(2)}) copy-start(bf16[2,512,1024]{2,1,0:T(8,128)(2,1)} %param.20) | copy-start | bytes 6291460
  537.2 173.6 %copy-start.36 = (f32[1,4,2,128]{3,1,2,0:T(4,128)S(1)}, f32[1,4,2,128]{3,1,2,0:T(4,128)}, u32[]{:S(2)}) copy-start(f32[1,4,2,128]{3,1,2,0:T(4,128)} %copy-done.35) | copy-start | bytes 12292
  537.2 173.6 %copy-start.38 = (f32[1,1024]{1,0:T(1,128)S(1)}, f32[1,1024]{1,0:T(1,128)}, u32[]{:S(2)}) copy-start(f32[1,1024]{1,0:T(1,128)} %copy-done.37) | copy-start | bytes 12292
  537.3 244.3 %all-reduce.28.cloned.1.call-start = ((), (), s32[]{:S(2)}) async-start(), calls=%async_computation.18 | async-start | bytes 6291456 | tf_op jit(solution)/shard_map/psum | solution.py:282
  539.7 174.3 %copy-start.45 = (f32[1,4,2,128]{3,1,2,0:T(4,128)S(1)}, f32[1,4,2,128]{3,1,2,0:T(4,128)}, u32[]{:S(2)}) copy-start(f32[1,4,2,128]{3,1,2,0:T(4,128)} %copy-done.44) | copy-start | bytes 12292
  539.7 174.3 %copy-start.48 = (f32[1024]{0:T(1024)S(1)}, f32[1024]{0:T(1024)}, u32[]{:S(2)}) copy-start(f32[1024]{0:T(1024)} %get-tuple-element.296) | copy-start | bytes 12292
  539.7 174.3 %copy-start.43 = (f32[1024]{0:T(1024)S(1)}, f32[1024]{0:T(1024)}, u32[]{:S(2)}) copy-start(f32[1024]{0:T(1024)} %copy-done.42) | copy-start | bytes 12292
  710.9 3.2 copy-start.9
  710.9 5.9 copy-start.47
  710.9 5.9 copy-start.56
  710.9 32.2 %copy-start.41 = (f32[1,1024]{1,0:T(1,128)S(1)}, f32[1,1024]{1,0:T(1,128)}, u32[]{:S(2)}) copy-start(f32[1,1024]{1,0:T(1,128)} %copy-done.40) | copy-start | bytes 12292
  710.9 32.2 %copy-start.49 = (f32[1,1024]{1,0:T(1,128)S(1)}, f32[1,1024]{1,0:T(1,128)}, u32[]{:S(2)}) copy-start(f32[1,1024]{1,0:T(1,128)} %get-tuple-element.445) | copy-start | bytes 12292
  781.6 7.2 copy-start.31
  (15 other events, 21.7 us)
Sparse Core Ops, SparseCore 0:
  10.1 29.8 all-gather.3
  139.5 86.2 all-reduce.21
  227.4 32.1 all-gather.5
  260.9 33.0 all-gather.7
  315.2 86.1 all-reduce.23
  414.8 13.6 reduce-scatter.6
  430.8 31.8 reduce-scatter.10
  465.0 31.8 reduce-scatter.8
  528.7 24.2 reduce-scatter.4
  555.8 155.0 all-reduce.25
  713.5 68.0 all-reduce.27
